TPU v7x, 32 devices: a whole 2x2x4 slice. The times are simulated.
32 devices in a mesh: seq: 4 (over y, x), exp: 8 (over z, core).
Axes of the slice: x: 2, y: 2, z: 4, core: 2. Of those that a mesh axis runs over, the one named last changes fastest.
Arguments:
- tokens: bfloat16 [2, 24576, 1024], P(None, ('seq', 'exp')), may hold values from -60 to 60
- router: bfloat16 [1024, 64], replicated, may hold values from -0.25 to 0.25
- w_in: bfloat16 [16, 1024, 4096], P('exp', None, 'seq'), may hold values from -0.1875 to 0.1875
- w_out: bfloat16 [16, 4096, 1024], P('exp', 'seq'), may hold values from -0.09375 to 0.09375
- grad_out: bfloat16 [2, 24576, 1024], P(None, ('seq', 'exp')), may hold values from -6 to 6
Outputs:
- mixed: bfloat16 [2, 24576, 1024], P(None, ('seq', 'exp'))
- grad_tokens: bfloat16 [2, 24576, 1024], P(None, ('seq', 'exp'))
- grad_router: float32 [1024, 64], P(('seq', 'exp'))
- grad_w_in: bfloat16 [16, 1024, 4096], P('exp', None, 'seq')
- grad_w_out: bfloat16 [16, 4096, 1024], P('exp', 'seq')
All inputs are finite; a program needn't handle non-finite values.
Results may differ from a plain program's by a relative error of at most 0.018.
Values may be sent and summed in bfloat16 or wider, within the bound.
A program may use at most 128 MiB of HBM per device.

v0:
```python
import jax
import jax.numpy as jnp
from jax import lax
from jax.sharding import PartitionSpec as P


def on_device(tokens, router, w_in, w_out, grad_out):
    clips, tok_rows, width = tokens.shape
    slot_total = router.shape[1]
    owned = slot_total // lax.axis_size("exp")
    experts_here = w_in.shape[0]
    per_expert = owned // experts_here
    logits = jnp.dot(
        tokens.reshape(clips * tok_rows, width), router, preferred_element_type=jnp.float32
    ).reshape(clips, tok_rows, slot_total)
    slot_peak = lax.pmax(jnp.max(logits, axis=1), ("seq", "exp"))
    exp_terms = jnp.exp(logits - slot_peak[:, None, :])
    slot_mass = lax.psum(jnp.sum(exp_terms, axis=1), ("seq", "exp"))
    dispatch = exp_terms / slot_mass[:, None, :]
    dispatch_b = dispatch.astype(jnp.bfloat16)
    mixing = jax.nn.softmax(logits, axis=2)
    mixing_b = mixing.astype(jnp.bfloat16)
    inputs = jnp.einsum("cts,ctd->scd", dispatch_b, tokens, preferred_element_type=jnp.float32)
    grads = jnp.einsum("cts,ctd->scd", mixing_b, grad_out, preferred_element_type=jnp.float32)
    summed = lax.psum(jnp.concatenate([inputs, grads], axis=1), ("seq", "exp"))
    owner_sums = lax.dynamic_slice_in_dim(summed, lax.axis_index("exp") * owned, owned, 0)
    expert_rows = (
        owner_sums[:, :clips].astype(jnp.bfloat16).reshape(experts_here, per_expert * clips, width)
    )
    grad_rows = (
        owner_sums[:, clips:].astype(jnp.bfloat16).reshape(experts_here, per_expert * clips, width)
    )
    pre = jnp.einsum("erd,edh->erh", expert_rows, w_in, preferred_element_type=jnp.float32)
    hidden = jax.nn.gelu(pre).astype(jnp.bfloat16)
    expert_part = jnp.einsum("erh,ehd->erd", hidden, w_out, preferred_element_type=jnp.float32)
    hidden_grad = jnp.einsum("erd,ehd->erh", grad_rows, w_out, preferred_element_type=jnp.float32)
    pre_grad = jax.vjp(jax.nn.gelu, pre)[1](hidden_grad)[0].astype(jnp.bfloat16)
    grad_w_out = jnp.einsum(
        "erh,erd->ehd", hidden, grad_rows, preferred_element_type=jnp.float32
    ).astype(jnp.bfloat16)
    grad_w_in = jnp.einsum(
        "erd,erh->edh", expert_rows, pre_grad, preferred_element_type=jnp.float32
    ).astype(jnp.bfloat16)
    input_part = jnp.einsum("erh,edh->erd", pre_grad, w_in, preferred_element_type=jnp.float32)
    out_sums, in_sums = (
        lax.psum(expert_part.astype(jnp.bfloat16), "seq").astype(jnp.float32),
        lax.psum(input_part.astype(jnp.bfloat16), "seq").astype(jnp.float32),
    )
    slot_outputs = out_sums.astype(jnp.bfloat16).reshape(owned, clips, width)
    slot_in_grads = in_sums.astype(jnp.bfloat16).reshape(owned, clips, width)
    shard_rows = lax.all_gather(slot_outputs, "exp", axis=0, tiled=True)
    weights = mixing_b
    outputs = jnp.einsum("cts,scd->ctd", weights, shard_rows, preferred_element_type=jnp.float32)
    block = jnp.einsum("ctd,scd->cts", grad_out, shard_rows, preferred_element_type=jnp.float32)
    mixed = outputs
    mixing_grad = block
    shard_rows = lax.all_gather(slot_in_grads, "exp", axis=0, tiled=True)
    weights = dispatch_b
    outputs = jnp.einsum("cts,scd->ctd", weights, shard_rows, preferred_element_type=jnp.float32)
    block = jnp.einsum("ctd,scd->cts", tokens, shard_rows, preferred_element_type=jnp.float32)
    inner = lax.psum(jnp.sum(dispatch * block, axis=1), ("seq", "exp"))
    logit_grad = dispatch * (block - inner[:, None, :]) + mixing * (
        mixing_grad - jnp.sum(mixing * mixing_grad, axis=2, keepdims=True)
    )
    logit_b = logit_grad.astype(jnp.bfloat16)
    router_part = jnp.dot(
        logit_b.reshape(clips * tok_rows, slot_total), router.T, preferred_element_type=jnp.float32
    ).reshape(clips, tok_rows, width)
    grad_tokens = (outputs + router_part).astype(jnp.bfloat16)
    grad_router = lax.psum_scatter(
        jnp.einsum("ctd,cts->ds", tokens, logit_b, preferred_element_type=jnp.float32),
        ("seq", "exp"),
        scatter_dimension=0,
        tiled=True,
    )
    return (mixed.astype(jnp.bfloat16), grad_tokens, grad_router, grad_w_in, grad_w_out)


def solution(mesh):
    return jax.shard_map(
        on_device,
        mesh=mesh,
        in_specs=(
            P(None, ("seq", "exp"), None),
            P(),
            P("exp", None, "seq"),
            P("exp", "seq", None),
            P(None, ("seq", "exp"), None),
        ),
        out_specs=(
            P(None, ("seq", "exp"), None),
            P(None, ("seq", "exp"), None),
            P(("seq", "exp"), None),
            P("exp", None, "seq"),
            P("exp", "seq", None),
        ),
        check_vma=False,
    )
```

profile of v0, /device:TPU:0, one launch (start us, length us, event | category | flops | bytes accessed | tf_op | source)
XLA Modules:
  0.0 442.6 jit_solution(9276342582157628203)
XLA Ops:
  7.2 0.0 copy-start
  7.2 0.0 all-reduce.4.cloned.1.call-start
  7.2 1.8 copy-done
  9.1 2.1 fusion.37
  11.1 0.8 fusion.36
  12.0 41.9 %pmax.7 = f32[2,64]{1,0:T(2,128)S(1)} all-reduce(f32[2,64]{1,0:T(2,128)S(1)} %get-tuple-element.26), channel_id=1, replica_groups=mesh['seq'=4,'exp'=8] {'seq','exp'}, use_global_device_ids=true, to_apply=%region_3.0 | all-reduce | flops 128 | bytes 1024 | tf_op jit(solution)/shard_map/pmax | solution.py:16
  53.9 0.8 fusion.13
  54.7 40.3 %psum.35 = f32[2,64]{1,0:T(2,128)S(1)} all-reduce(f32[2,64]{1,0:T(2,128)} %fusion.13), channel_id=1, replica_groups=mesh['seq'=4,'exp'=8] {'seq','exp'}, use_global_device_ids=true, to_apply=%region_5.0 | all-reduce | flops 128 | bytes 1024 | tf_op jit(solution)/shard_map/psum | solution.py:18
  95.0 1.5 convolution_bitcast_fusion.1
  96.5 3.4 convolution_bitcast_fusion
  99.9 2.4 pad_maximum_fusion
  102.3 49.9 %all-reduce.5 = bf16[64,4,1024]{2,0,1:T(8,128)(2,1)} all-reduce(f32[64,4,1024]{2,0,1:T(8,128)} %pad_maximum_fusion), channel_id=1, replica_groups=mesh['seq'=4,'exp'=8] {'seq','exp'}, use_global_device_ids=true, to_apply=%region_6.0 | all-reduce | flops 262144 | bytes 1572864 | tf_op jit(solution)/shard_map/psum | solution.py:25
  152.2 0.8 dynamic-slice_convert_fusion
  153.0 0.6 fusion.35
  153.6 0.6 copy.20
  154.3 1.4 reshape.38
  155.7 1.4 copy.18
  157.1 1.4 reshape.36
  158.4 0.0 copy-start.6
  158.4 0.0 copy-start.1
  158.4 3.5 fusion.38
  162.0 0.0 copy-done.6
  162.0 3.5 fusion.28
  165.5 0.0 copy-start.4
  165.5 0.6 copy-done.4
  166.1 0.0 copy-done.1
  166.1 1.3 convolution_convert_fusion.4
  167.4 1.4 reshape.37
  168.8 1.4 copy.19
  170.1 4.0 convolution_convert_fusion.3
  174.2 1.4 reshape.39
  175.5 1.4 copy.21
  176.9 0.0 all-reduce.4.cloned.1.call-update
  176.9 0.0 reduce-scatter.4.cloned.1.call-start
  177.0 0.0 copy-start.5
  177.0 0.0 copy-start.7
  177.0 4.2 convolution_convert_fusion
  181.2 0.0 copy-done.5
  181.2 0.0 copy-done.7
  181.2 3.3 convolution_convert_fusion.1
  184.5 33.1 %all-reduce.4.cloned.1.call-done = (bf16[8,2,1024]{2,0,1:T(8,128)(2,1)}, bf16[8,2,1024]{2,0,1:T(8,128)(2,1)}) async-done(((bf16[8,2,1024]{2,0,1:T(8,128)(2,1)}, bf16[8,2,1024]{2,0,1:T(8,128)(2,1)}), (bf16[8,2,1024]{2,0,1:T(8,128)(2,1)}, bf16[8,2,1024]{2,0,1:T(8,128)(2,1)})) %all-reduce.4.cloned.1.call-update) | async-done | bytes 65552 | tf_op jit(solution)/shard_map/psum | solution.py:46
  217.6 14.6 %all_gather.7 = bf16[64,2,1024]{2,0,1:T(8,128)(2,1)S(1)} all-gather(bf16[8,2,1024]{2,0,1:T(8,128)(2,1)} %get-tuple-element.21), channel_id=1, replica_groups=mesh['seq'=4,'exp'=8] {'exp'}, dimensions={0}, use_global_device_ids=true | all-gather | bytes 294912 | tf_op jit(solution)/shard_map/all_gather | solution.py:57
  232.2 0.0 copy-start.8
  232.2 0.0 copy-start.2
  232.2 3.8 fusion.17
  236.0 2.4 multiply_reduce_fusion.1
  238.4 0.0 copy-done.8
  238.4 14.2 %all_gather.6 = bf16[64,2,1024]{2,0,1:T(8,128)(2,1)S(1)} all-gather(bf16[8,2,1024]{2,0,1:T(8,128)(2,1)S(1)} %copy-done.8), channel_id=1, replica_groups=mesh['seq'=4,'exp'=8] {'exp'}, dimensions={0}, use_global_device_ids=true | all-gather | bytes 294912 | tf_op jit(solution)/shard_map/all_gather | solution.py:51
  252.6 0.0 copy-done.2
  252.6 0.0 copy-start.3
  252.6 1.8 convolution_bitcast_fusion.2
  254.4 0.0 copy-done.3
  254.4 39.4 %psum.39 = f32[2,64]{1,0:T(2,128)} all-reduce(f32[2,64]{1,0:T(2,128)} %get-tuple-element.30), channel_id=1, replica_groups=mesh['seq'=4,'exp'=8] {'seq','exp'}, use_global_device_ids=true, to_apply=%region_10.0 | all-reduce | flops 128 | bytes 1024 | tf_op jit(solution)/shard_map/psum | solution.py:61
  293.8 3.0 convolution_bitcast_fusion.4
  296.8 2.0 copy.23
  298.8 0.0 reduce-scatter.4.cloned.1.call-update
  298.8 3.7 convolution_convert_fusion.2
  302.5 6.2 %add_convert_fusion = bf16[2,768,1024]{2,1,0:T(8,128)(2,1)} fusion(f32[2,768,1024]{2,1,0:T(8,128)} %fusion.17, f32[2,768,64]{1,2,0:T(8,128)} %convolution_bitcast_fusion.2, f32[2,768,64]{1,2,0:T(8,128)} %get-tuple-element.31, f32[2,64]{1,0:T(2,128)} %psum.39, bf16[1024,64]{0,1:T(8,128)(2,1)} %param.6, f32[2,768,64]{1,2,0:T(8,128)} %get-tuple-element.25, ...), kind=kOutput, calls=%fused_computation.2 | convolution fusion | flops 205555264 | bytes 11148800 | tf_op jit(solution)/shard_map/dot_general | solution.py:66
  308.7 127.1 %reduce-scatter.4.cloned.1.call-done = f32[32,64]{1,0:T(8,128)} async-done(((f32[1024,64]{1,0:T(8,128)}), f32[32,64]{1,0:T(8,128)}) %reduce-scatter.4.cloned.1.call-update) | async-done | bytes 8208
Async XLA Ops:
  7.2 1.9 copy-start
  7.2 210.4 %all-reduce.4.cloned.1.call-start = ((), (), s32[]{:S(2)}) async-start(), calls=%async_computation.2 | async-start | bytes 131072 | tf_op jit(solution)/shard_map/psum | solution.py:46
  158.4 3.5 copy-start.6
  158.4 7.7 %copy-start.1 = (bf16[2,1024,1024]{2,1,0:T(8,128)(2,1)S(1)}, bf16[2,1024,1024]{2,1,0:T(8,128)(2,1)}, u32[]{:S(2)}) copy-start(bf16[2,1024,1024]{2,1,0:T(8,128)(2,1)} %param.8) | copy-start | bytes 12582916
  165.5 0.6 copy-start.4
  176.9 258.9 %reduce-scatter.4.cloned.1.call-start = ((), (), s32[]{:S(2)}) async-start(), calls=%async_computation.1 | async-start | bytes 540672
  177.0 4.2 copy-start.5
  177.0 4.2 copy-start.7
  232.2 6.2 %copy-start.8 = (bf16[8,2,1024]{2,0,1:T(8,128)(2,1)S(1)}, bf16[8,2,1024]{2,0,1:T(8,128)(2,1)}, u32[]{:S(2)}) copy-start(bf16[8,2,1024]{2,0,1:T(8,128)(2,1)} %get-tuple-element.20) | copy-start | bytes 98308
  232.2 20.4 %copy-start.2 = (bf16[2,768,1024]{2,1,0:T(8,128)(2,1)S(1)}, bf16[2,768,1024]{2,1,0:T(8,128)(2,1)}, u32[]{:S(2)}) copy-start(bf16[2,768,1024]{2,1,0:T(8,128)(2,1)} %param.9) | copy-start | bytes 9437188
  252.6 1.8 copy-start.3
Sparse Core Ops, SparseCore 0:
  177.0 40.5 all-reduce.3
  298.9 136.8 reduce-scatter.3
where the time goes:
time: 444 us; the launch traced here: 443 us
  blocking collectives  200 us (45%)
  waiting for transfers between devices  160 us (36%)
  matrix products  47.6 us (11%)
  local copies, waits for them, and re-layouts  16.2 us (4%)
  between operations  14.1 us (3%)
    unnamed x3, waiting for transfers between devices  127 us
    psum x1, blocking collectives, on_device(): summed = lax.psum(jnp.concatenate([inputs, grads], axis=1), ('seq', 'exp'))  49.9 us
    pmax x1, blocking collectives, on_device(): slot_peak = lax.pmax(jnp.max(logits, axis=1), ('seq', 'exp'))  41.9 us
    psum x1, blocking collectives, on_device(): slot_mass = lax.psum(jnp.sum(exp_terms, axis=1), ('seq', 'exp'))  40.3 us
    psum x1, blocking collectives, on_device(): inner = lax.psum(jnp.sum(dispatch * block, axis=1), ('seq', 'exp'))  39.4 us
    psum x1, waiting for transfers between devices, on_device(): lax.psum(expert_part.astype(jnp.bfloat16), 'seq').astype(jnp.float32)  33.1 us
    all_gather x1, blocking collectives, on_device(): shard_rows = lax.all_gather(slot_in_grads, 'exp', axis=0, tiled=True)  14.6 us
    all_gather x1, blocking collectives, on_device(): shard_rows = lax.all_gather(slot_outputs, 'exp', axis=0, tiled=True)  14.2 us
  transfers between devices with their start and end apart: 2, of which 2 were waited for; matrix products, arithmetic and copies ran while one was open for 4% of the time, Pallas kernels for 0%

commit v1 on v0

--- a/solution.py
+++ b/solution.py
@@ -1,7 +1,16 @@
+import functools
 import jax
 import jax.numpy as jnp
 from jax import lax
 from jax.sharding import PartitionSpec as P
+
+
+def recast_indices(base_x, axis_id):
+    taken_in = lax.all_gather(base_x, axis_id).sum(axis=0)
+    return taken_in
+
+
+save_links = functools.partial(recast_indices, axis_id=("seq", "exp"))
 
 
 def on_device(tokens, router, w_in, w_out, grad_out):
@@ -58,7 +67,7 @@
     weights = dispatch_b
     outputs = jnp.einsum("cts,scd->ctd", weights, shard_rows, preferred_element_type=jnp.float32)
     block = jnp.einsum("ctd,scd->cts", tokens, shard_rows, preferred_element_type=jnp.float32)
-    inner = lax.psum(jnp.sum(dispatch * block, axis=1), ("seq", "exp"))
+    inner = save_links(jnp.sum(dispatch * block, axis=1))
     logit_grad = dispatch * (block - inner[:, None, :]) + mixing * (
         mixing_grad - jnp.sum(mixing * mixing_grad, axis=2, keepdims=True)
     )

time: 444 us -> 445 us (level)
    all_gather x0 -> x1, blocking collectives: none -> 43.1 us  [recast_indices(): taken_in = lax.all_gather(base_x, axis_id).sum(axis=0)]
    psum x1 -> x0, blocking collectives: 39.4 us -> none  [on_device(): inner = lax.psum(jnp.sum(dispatch * block, axis=1), ('seq', 'exp'))]
where the time goes in v1:
time: 445 us; the launch traced here: 443 us
  blocking collectives  204 us (46%)
  waiting for transfers between devices  156 us (35%)
  matrix products  47.1 us (11%)
  local copies, waits for them, and re-layouts  16.2 us (4%)
  between operations  14.1 us (3%)
  other arithmetic  5.42 us (1%)
    unnamed x3, waiting for transfers between devices  123 us
    psum x1, blocking collectives, on_device(): summed = lax.psum(jnp.concatenate([inputs, grads], axis=1), ('seq', 'exp'))  49.9 us
    all_gather x1, blocking collectives, recast_indices(): taken_in = lax.all_gather(base_x, axis_id).sum(axis=0)  43.1 us
    pmax x1, blocking collectives, on_device(): slot_peak = lax.pmax(jnp.max(logits, axis=1), ('seq', 'exp'))  41.9 us
    psum x1, blocking collectives, on_device(): slot_mass = lax.psum(jnp.sum(exp_terms, axis=1), ('seq', 'exp'))  40.3 us
    psum x1, waiting for transfers between devices, on_device(): lax.psum(expert_part.astype(jnp.bfloat16), 'seq').astype(jnp.float32)  33.1 us
    all_gather x1, blocking collectives, on_device(): shard_rows = lax.all_gather(slot_in_grads, 'exp', axis=0, tiled=True)  14.6 us
    all_gather x1, blocking collectives, on_device(): shard_rows = lax.all_gather(slot_outputs, 'exp', axis=0, tiled=True)  14.2 us
  transfers between devices with their start and end apart: 2, of which 2 were waited for; matrix products, arithmetic and copies ran while one was open for 4% of the time, Pallas kernels for 0%

profile of v1, /device:TPU:0, one launch (start us, length us, event | category | flops | bytes accessed | tf_op | source)
XLA Modules:
  0.0 443.2 jit_solution(3502107462263146335)
XLA Ops:
  7.2 0.0 copy-start
  7.2 0.0 all-reduce.4.cloned.1.call-start
  7.2 1.8 copy-done
  9.1 2.1 fusion.37
  11.1 0.8 fusion.36
  12.0 41.9 %pmax.7 = f32[2,64]{1,0:T(2,128)S(1)} all-reduce(f32[2,64]{1,0:T(2,128)S(1)} %get-tuple-element.26), channel_id=1, replica_groups=mesh['seq'=4,'exp'=8] {'seq','exp'}, use_global_device_ids=true, to_apply=%region_3.0 | all-reduce | flops 128 | bytes 1024 | tf_op jit(solution)/shard_map/pmax | solution.py:25
  53.9 0.8 fusion.13
  54.7 40.3 %psum.28 = f32[2,64]{1,0:T(2,128)S(1)} all-reduce(f32[2,64]{1,0:T(2,128)} %fusion.13), channel_id=1, replica_groups=mesh['seq'=4,'exp'=8] {'seq','exp'}, use_global_device_ids=true, to_apply=%region_5.0 | all-reduce | flops 128 | bytes 1024 | tf_op jit(solution)/shard_map/psum | solution.py:27
  95.0 1.5 convolution_bitcast_fusion.1
  96.5 3.4 convolution_bitcast_fusion
  99.9 2.4 pad_maximum_fusion
  102.3 49.9 %all-reduce.5 = bf16[64,4,1024]{2,0,1:T(8,128)(2,1)} all-reduce(f32[64,4,1024]{2,0,1:T(8,128)} %pad_maximum_fusion), channel_id=1, replica_groups=mesh['seq'=4,'exp'=8] {'seq','exp'}, use_global_device_ids=true, to_apply=%region_6.0 | all-reduce | flops 262144 | bytes 1572864 | tf_op jit(solution)/shard_map/psum | solution.py:34
  152.2 0.8 dynamic-slice_convert_fusion
  153.0 0.6 fusion.35
  153.6 0.6 copy.20
  154.3 1.4 reshape.38
  155.7 1.4 copy.18
  157.1 1.4 reshape.36
  158.4 0.0 copy-start.6
  158.4 0.0 copy-start.1
  158.4 3.5 fusion.38
  162.0 0.0 copy-done.6
  162.0 3.5 fusion.28
  165.5 0.0 copy-start.4
  165.5 0.6 copy-done.4
  166.1 0.0 copy-done.1
  166.1 1.3 convolution_convert_fusion.4
  167.4 1.4 reshape.37
  168.8 1.4 copy.19
  170.1 4.0 convolution_convert_fusion.3
  174.2 1.4 reshape.39
  175.5 1.4 copy.21
  176.9 0.0 all-reduce.4.cloned.1.call-update
  176.9 0.0 reduce-scatter.4.cloned.1.call-start
  177.0 0.0 copy-start.5
  177.0 0.0 copy-start.7
  177.0 4.2 convolution_convert_fusion
  181.2 0.0 copy-done.5
  181.2 0.0 copy-done.7
  181.2 3.3 convolution_convert_fusion.1
  184.5 33.1 %all-reduce.4.cloned.1.call-done = (bf16[8,2,1024]{2,0,1:T(8,128)(2,1)}, bf16[8,2,1024]{2,0,1:T(8,128)(2,1)}) async-done(((bf16[8,2,1024]{2,0,1:T(8,128)(2,1)}, bf16[8,2,1024]{2,0,1:T(8,128)(2,1)}), (bf16[8,2,1024]{2,0,1:T(8,128)(2,1)}, bf16[8,2,1024]{2,0,1:T(8,128)(2,1)})) %all-reduce.4.cloned.1.call-update) | async-done | bytes 65552 | tf_op jit(solution)/shard_map/psum | solution.py:55
  217.6 14.6 %all_gather.13 = bf16[64,2,1024]{2,0,1:T(8,128)(2,1)S(1)} all-gather(bf16[8,2,1024]{2,0,1:T(8,128)(2,1)} %get-tuple-element.21), channel_id=1, replica_groups=mesh['seq'=4,'exp'=8] {'exp'}, dimensions={0}, use_global_device_ids=true | all-gather | bytes 294912 | tf_op jit(solution)/shard_map/all_gather | solution.py:66
  232.2 0.0 copy-start.8
  232.2 0.0 copy-start.2
  232.2 3.8 fusion.17
  236.0 1.8 multiply_reduce_fusion.1
  237.8 0.0 copy-done.8
  237.8 14.2 %all_gather.12 = bf16[64,2,1024]{2,0,1:T(8,128)(2,1)S(1)} all-gather(bf16[8,2,1024]{2,0,1:T(8,128)(2,1)S(1)} %copy-done.8), channel_id=1, replica_groups=mesh['seq'=4,'exp'=8] {'exp'}, dimensions={0}, use_global_device_ids=true | all-gather | bytes 294912 | tf_op jit(solution)/shard_map/all_gather | solution.py:60
  252.1 0.0 copy-done.2
  252.1 0.0 copy-start.3
  252.1 1.8 convolution_bitcast_fusion.2
  253.9 0.0 copy-done.3
  253.9 43.1 %all-gather.1 = f32[32,2,64]{2,1,0:T(2,128)} all-gather(f32[1,2,64]{2,1,0:T(2,128)S(1)} %bitcast.44), channel_id=2, replica_groups=mesh['seq'=4,'exp'=8] {'seq','exp'}, dimensions={0}, use_global_device_ids=true | all-gather | bytes 16896 | tf_op jit(solution)/shard_map/all_gather | solution.py:9
  297.0 1.4 reduce_sum.48
  298.4 3.0 convolution_bitcast_fusion.4
  301.4 2.0 copy.23
  303.3 0.0 reduce-scatter.4.cloned.1.call-update
  303.4 3.7 convolution_convert_fusion.2
  307.0 6.2 %add_convert_fusion = bf16[2,768,1024]{2,1,0:T(8,128)(2,1)} fusion(f32[2,768,1024]{2,1,0:T(8,128)} %fusion.17, f32[2,768,64]{1,2,0:T(8,128)} %convolution_bitcast_fusion.2, f32[2,768,64]{1,2,0:T(8,128)} %get-tuple-element.31, f32[2,64]{1,0:T(2,128)} %reduce_sum.48, bf16[1024,64]{0,1:T(8,128)(2,1)} %param.6, f32[2,768,64]{1,2,0:T(8,128)} %get-tuple-element.25, ...), kind=kOutput, calls=%fused_computation.2 | convolution fusion | flops 205555264 | bytes 11148800 | tf_op jit(solution)/shard_map/dot_general | solution.py:75
  313.3 123.1 %reduce-scatter.4.cloned.1.call-done = f32[32,64]{1,0:T(8,128)} async-done(((f32[1024,64]{1,0:T(8,128)}), f32[32,64]{1,0:T(8,128)}) %reduce-scatter.4.cloned.1.call-update) | async-done | bytes 8208
Async XLA Ops:
  7.2 1.9 copy-start
  7.2 210.4 %all-reduce.4.cloned.1.call-start = ((), (), s32[]{:S(2)}) async-start(), calls=%async_computation.2 | async-start | bytes 131072 | tf_op jit(solution)/shard_map/psum | solution.py:55
  158.4 3.5 copy-start.6
  158.4 7.7 %copy-start.1 = (bf16[2,1024,1024]{2,1,0:T(8,128)(2,1)S(1)}, bf16[2,1024,1024]{2,1,0:T(8,128)(2,1)}, u32[]{:S(2)}) copy-start(bf16[2,1024,1024]{2,1,0:T(8,128)(2,1)} %param.8) | copy-start | bytes 12582916
  165.5 0.6 copy-start.4
  176.9 259.4 %reduce-scatter.4.cloned.1.call-start = ((), (), s32[]{:S(2)}) async-start(), calls=%async_computation.1 | async-start | bytes 540672
  177.0 4.2 copy-start.5
  177.0 4.2 copy-start.7
  232.2 5.6 %copy-start.8 = (bf16[8,2,1024]{2,0,1:T(8,128)(2,1)S(1)}, bf16[8,2,1024]{2,0,1:T(8,128)(2,1)}, u32[]{:S(2)}) copy-start(bf16[8,2,1024]{2,0,1:T(8,128)(2,1)} %get-tuple-element.20) | copy-start | bytes 98308
  232.2 19.8 %copy-start.2 = (bf16[2,768,1024]{2,1,0:T(8,128)(2,1)S(1)}, bf16[2,768,1024]{2,1,0:T(8,128)(2,1)}, u32[]{:S(2)}) copy-start(bf16[2,768,1024]{2,1,0:T(8,128)(2,1)} %param.9) | copy-start | bytes 9437188
  252.1 1.8 copy-start.3
Sparse Core Ops, SparseCore 0:
  177.0 40.5 all-reduce.3
  303.5 132.8 reduce-scatter.3
